TPU v7x, 32 devices: a whole 2x2x4 slice. The times are simulated.
32 devices in a mesh: frame: 4 (over x, core), rank: 8 (over z, y).
Axes of the slice: x: 2, y: 2, z: 4, core: 2. Of those that a mesh axis runs over, the one named last changes fastest.
Arguments:
- layers: float32 [4, 8, 4, 32, 16384], P('frame', 'rank')
- depth_order: int32 [4, 8], P('frame'), may hold values from 0 to 7, as said below
- tile_slots: int32 [32], replicated, may hold values from 0 to 31, each once
Outputs:
- filtered: float32 [32, 4, 4, 16384], P('frame', None, None, 'rank')
- coverage: float32 [4], P('frame')
Inputs may be any that keep to these rules, and one draw needn't show every extreme that they name: `depth_order`: each row is a permutation of the ranks in which, for every bit b, the ranks that agree on all bits from b upward take consecutive depths. `tile_slots`: slot s belongs to frame group s // 8.
All inputs are finite; a program needn't handle non-finite values.
Results may differ from a plain program's by a relative error of at most 0.00002.
Values sent between devices are 32-bit elements; how exact they have to be, the bound alone decides.
No kernel may reach another device: no remote copies, remote signals or barrier semaphores. Data moves between devices by JAX's collectives and lax.ppermute only.
A program may use at most 64 MiB of HBM per device.

v0:
```python
import jax
import jax.numpy as jnp
from jax import lax
from jax.sharding import PartitionSpec as P


def smooth_frames(block):
    before = jnp.concatenate([block[:, :, :1], block[:, :, :-1]], axis=2)
    after = jnp.concatenate([block[:, :, 1:], block[:, :, -1:]], axis=2)
    return 0.25 * before + 0.5 * block + 0.25 * after


def shards(layers, depth_order, tile_slots):
    mine = layers[0, 0]
    order = depth_order[0]
    ranks = lax.axis_size("rank")
    groups = lax.axis_size("frame")
    channels, tile_count, pixels = mine.shape
    piece = pixels // ranks
    blocks = mine.reshape(channels, tile_count, ranks, piece)
    gathered = lax.all_to_all(blocks, "rank", split_axis=2, concat_axis=2, tiled=True)

    def step(total, rank_id):
        layer = lax.dynamic_index_in_dim(gathered, rank_id, 2, keepdims=False)
        return (total + (1.0 - total[3:4]) * layer, None)

    start = jnp.zeros((gathered.shape[0], gathered.shape[1], gathered.shape[3]), jnp.float32)
    total, unused = lax.scan(step, start, order)
    opacity = lax.psum(jnp.sum(total[3]), "rank")
    coverage = (opacity / (tile_count * pixels)).reshape(1)
    picked = jnp.transpose(total[:, tile_slots, :], (1, 0, 2))
    per_group = tile_count // groups
    picked = picked.reshape(groups, per_group, 1, channels, piece)
    filtered = smooth_frames(
        lax.all_to_all(picked, "frame", split_axis=0, concat_axis=2, tiled=True)
    )
    filtered = filtered.reshape(per_group, groups, channels, piece)
    return (filtered, coverage)


def solution(mesh):
    placed = (P("frame", "rank", None, None, None), P("frame", None), P())
    return jax.shard_map(
        shards,
        mesh=mesh,
        in_specs=placed,
        out_specs=(P("frame", None, None, "rank"), P("frame")),
        check_vma=False,
    )
```

profile of v0, /device:TPU:0, one launch (start us, length us, event | category | flops | bytes accessed | tf_op | source)
XLA Modules:
  0.0 275.3 jit_solution(9798022142263179095)
XLA Ops:
  0.6 9.9 %copy.20 = f32[16,8,8,2048]{3,2,1,0:T(8,128)S(1)} copy(f32[16,8,8,2048]{3,1,2,0:T(8,128)} %bitcast.42) | data formatting | bytes 16777216
  10.5 8.1 %copy.13 = f32[4,32,8,2048]{3,1,0,2:T(8,128)} copy(f32[4,32,8,2048]{3,2,1,0:T(8,128)S(1)} %bitcast.39) | data formatting | bytes 16777216 | tf_op jit(solution)/shard_map/reshape;squeeze | solution.py:20
  18.6 7.6 %all-to-all-start = ((f32[4,32,8,2048]{3,1,0,2:T(8,128)}), f32[4,32,8,2048]{3,1,0,2:T(8,128)}, u32[]{:S(2)}, u32[]{:S(2)}) async-start(f32[4,32,8,2048]{3,1,0,2:T(8,128)} %copy.13), calls=%async_computation | async-start | bytes 16777216 | tf_op jit(solution)/shard_map/all_to_all | solution.py:21
  26.2 183.1 %all-to-all-done = f32[4,32,8,2048]{3,1,0,2:T(8,128)} async-done(((f32[4,32,8,2048]{3,1,0,2:T(8,128)}), f32[4,32,8,2048]{3,1,0,2:T(8,128)}, u32[]{:S(2)}, u32[]{:S(2)}) %all-to-all-start) | async-done | bytes 8388640 | tf_op jit(solution)/shard_map/all_to_all | solution.py:21
  209.4 34.3 %while.11 = (s32[]{:T(128)}, f32[4,32,2048]{2,1,0:T(8,128)S(1)}, s32[8]{0:T(128)S(1)}, f32[4,32,8,2048]{3,1,0,2:T(8,128)}, s32[]{:T(128)}, /*index=5*/s32[]{:T(128)}, s32[]{:T(128)}) while((s32[]{:T(128)}, f32[4,32,2048]{2,1,0:T(8,128)S(1)}, s32[8]{0:T(128)S(1)}, f32[4,32,8,2048]{3,1,0,2:T(8,128)}, s32[]{:T(128)}, ...), condition=%wide.region_1.2_spmd.clone, body=%wide.region_0.1_spmd.clone.sunk | while | flops 1114118 | bytes 6029450 | solution.py:28
  209.4 0.6 dynamic_slice.14
  212.0 1.6 fusion.7
  213.7 0.6 dynamic_slice.14
  216.2 0.1 broadcast_select_fusion.2
  216.3 1.6 fusion.7
  217.9 0.6 dynamic_slice.14
  220.5 0.1 broadcast_select_fusion.2
  220.6 1.6 fusion.7
  222.2 0.6 dynamic_slice.14
  224.9 1.6 fusion.7
  226.5 0.6 dynamic_slice.14
  229.2 1.6 fusion.7
  230.8 0.6 dynamic_slice.14
  233.5 1.6 fusion.7
  235.1 0.6 dynamic_slice.14
  237.8 1.6 fusion.7
  239.4 0.6 dynamic_slice.14
  242.1 1.6 fusion.7
  243.7 0.7 copy.14
  244.4 1.2 gather_fusion
  245.5 1.6 copy.16
  247.1 3.5 %all-to-all-start.1 = ((f32[4,8,1,4,2048]{4,1,3,2,0:T(8,128)}), f32[4,8,1,4,2048]{4,1,3,2,0:T(8,128)S(1)}, u32[]{:S(2)}, u32[]{:S(2)}) async-start(f32[4,8,1,4,2048]{4,1,3,2,0:T(8,128)} %copy.16), calls=%async_computation.1 | async-start | bytes 2097152 | tf_op jit(solution)/shard_map/all_to_all | solution.py:35
  250.6 0.7 slice_reduce_fusion
  251.3 20.1 %psum.7 = f32[]{:T(128)} all-reduce(f32[]{:T(128)} %slice_reduce_fusion), channel_id=1, replica_groups=mesh['frame'=4,'rank'=8] {'rank'}, use_global_device_ids=true, to_apply=%region_3.4 | all-reduce | flops 1 | bytes 8 | tf_op jit(solution)/shard_map/psum | solution.py:29
  272.1 0.2 slice_bitcast_fusion
  272.3 0.3 fusion.3
  272.6 1.6 copy.17
  (23 shorter events, 0.8 us)
Async XLA Ops:
  18.6 7.6 %copy-start = (s32[32]{0:T(128)S(1)}, s32[32]{0:T(128)}, u32[]{:S(2)}) copy-start(s32[32]{0:T(128)} %param.7) | copy-start | bytes 388
  18.6 190.8 %copy-start.1 = (s32[1,8]{1,0:T(1,128)S(1)}, s32[1,8]{1,0:T(1,128)}, u32[]{:S(2)}) copy-start(s32[1,8]{1,0:T(1,128)} %param.6) | copy-start | bytes 100
  18.6 190.8 %all-to-all-start = ((f32[4,32,8,2048]{3,1,0,2:T(8,128)}), f32[4,32,8,2048]{3,1,0,2:T(8,128)}, u32[]{:S(2)}, u32[]{:S(2)}) async-start(f32[4,32,8,2048]{3,1,0,2:T(8,128)} %copy.13), calls=%async_computation | async-start | bytes 16777216 | tf_op jit(solution)/shard_map/all_to_all | solution.py:21
  247.1 24.9 %all-to-all-start.1 = ((f32[4,8,1,4,2048]{4,1,3,2,0:T(8,128)}), f32[4,8,1,4,2048]{4,1,3,2,0:T(8,128)S(1)}, u32[]{:S(2)}, u32[]{:S(2)}) async-start(f32[4,8,1,4,2048]{4,1,3,2,0:T(8,128)} %copy.16), calls=%async_computation.1 | async-start | bytes 2097152 | tf_op jit(solution)/shard_map/all_to_all | solution.py:35
where the time goes:
time: 276 us; the launch traced here: 275 us
  waiting for transfers between devices  183 us (66%)
  local copies, waits for them, and re-layouts  27.9 us (10%)
  blocking collectives  20.1 us (7%)
  loops' own time  15.9 us (6%)
  other arithmetic  14.7 us (5%)
  starting transfers between devices  11.1 us (4%)
    all_to_all x1, waiting for transfers between devices, shards(): lax.all_to_all(blocks, 'rank', split_axis=2, concat_axis=2, tiled=True)  183 us
    psum x1, blocking collectives, shards(): opacity = lax.psum(jnp.sum(total[3]), 'rank')  20.1 us
    another operation x1, loops' own time, shards(): total, unused = lax.scan(step, start, order)  15.9 us
    add x8, other arithmetic, step(): return (total + (1.0 - total[3:4]) * layer, None)  12.8 us
    unnamed x6, local copies, waits for them, and re-layouts  11.5 us
    another operation x1, local copies, waits for them, and re-layouts, shards(): blocks = mine.reshape(channels, tile_count, ranks, piece)  8.08 us
    all_to_all x1, starting transfers between devices, shards(): lax.all_to_all(blocks, 'rank', split_axis=2, concat_axis=2, tiled=True)  7.62 us
  transfers between devices with their start and end apart: 2, of which 1 were waited for; matrix products, arithmetic and copies ran while one was open for 0% of the time, Pallas kernels for 0%

commit v1 on v0

--- a/solution.py
+++ b/solution.py
@@ -18,7 +18,10 @@
     channels, tile_count, pixels = mine.shape
     piece = pixels // ranks
     blocks = mine.reshape(channels, tile_count, ranks, piece)
-    gathered = lax.all_to_all(blocks, "rank", split_axis=2, concat_axis=2, tiled=True)
+    gathered = jnp.concatenate(
+        lax.all_to_all(jnp.stack(jnp.split(blocks, lax.axis_size("rank"), axis=2)), "rank", 0, 0),
+        axis=2,
+    )
 
     def step(total, rank_id):
         layer = lax.dynamic_index_in_dim(gathered, rank_id, 2, keepdims=False)

time: 276 us -> 295 us (1.069)
  local copies, waits for them, and re-layouts: 27.9 us -> 47.4 us
    unnamed x6 -> x14, local copies, waits for them, and re-layouts: 11.5 us -> 37 us
    another operation x1, local copies, waits for them, and re-layouts: 8.08 us -> 2.12 us  [shards(): jnp.stack(jnp.split(blocks, lax.axis_size('rank'), axis=2))]
where the time goes in v1:
time: 295 us
  waiting for transfers between devices  183 us (62%)
  local copies, waits for them, and re-layouts  47.4 us (16%)
  blocking collectives  20.1 us (7%)
  loops' own time  15.9 us (5%)
  other arithmetic  14.6 us (5%)
  starting transfers between devices  11 us (4%)
    all_to_all x1, waiting for transfers between devices, shards(): lax.all_to_all(jnp.stack(jnp.split(blocks, lax.axis_size('rank'), axis=2)...  183 us
    unnamed x14, local copies, waits for them, and re-layouts  37 us
    psum x1, blocking collectives, shards(): opacity = lax.psum(jnp.sum(total[3]), 'rank')  20.1 us
    another operation x1, loops' own time, shards(): total, unused = lax.scan(step, start, order)  15.9 us
    add x8, other arithmetic, step(): return (total + (1.0 - total[3:4]) * layer, None)  12.8 us
    all_to_all x1, starting transfers between devices, shards(): lax.all_to_all(jnp.stack(jnp.split(blocks, lax.axis_size('rank'), axis=2)...  7.44 us
  transfers between devices with their start and end apart: 2, of which 1 were waited for; matrix products, arithmetic and copies ran while one was open for 0% of the time, Pallas kernels for 0%

profile of v1, /device:TPU:0, one launch (start us, length us, event | category | flops | bytes accessed | tf_op | source)
XLA Modules:
  0.0 294.5 jit_solution(8123978883865519611)
XLA Ops:
  0.6 9.9 %copy.26 = f32[16,8,8,2048]{3,2,1,0:T(8,128)S(1)} copy(f32[16,8,8,2048]{3,1,2,0:T(8,128)} %bitcast.86) | data formatting | bytes 16777216
  10.5 1.7 fusion.9
  12.2 2.1 fusion.8
  14.3 2.1 fusion.7
  16.5 2.1 fusion.6
  18.6 2.2 fusion.5
  20.8 2.3 fusion.4
  23.1 2.1 fusion.3
  25.2 2.1 fusion.2
  27.3 7.4 %all-to-all-start = ((f32[8,4,32,1,2048]{4,3,2,1,0:T(1,128)}), f32[8,4,32,1,2048]{4,3,2,1,0:T(1,128)}, u32[]{:S(2)}, u32[]{:S(2)}) async-start(f32[8,4,32,1,2048]{4,3,2,1,0:T(1,128)} %fusion.2), calls=%async_computation | async-start | bytes 16777216 | tf_op jit(solution)/shard_map/all_to_all | solution.py:22
  34.8 183.1 %all-to-all-done = f32[8,4,32,1,2048]{4,3,2,1,0:T(1,128)} async-done(((f32[8,4,32,1,2048]{4,3,2,1,0:T(1,128)}), f32[8,4,32,1,2048]{4,3,2,1,0:T(1,128)}, u32[]{:S(2)}, u32[]{:S(2)}) %all-to-all-start) | async-done | bytes 8388640 | tf_op jit(solution)/shard_map/all_to_all | solution.py:22
  217.9 10.7 %copy.28 = f32[4,32,8,1,2048]{4,1,3,0,2:T(8,128)} copy(f32[4,32,8,1,2048]{4,3,1,0,2:T(1,128)} %bitcast.9) | data formatting | bytes 16777216
  228.7 34.2 %while.11 = (s32[]{:T(128)}, f32[4,32,2048]{2,1,0:T(8,128)S(1)}, s32[8]{0:T(128)S(1)}, f32[4,32,8,2048]{3,1,0,2:T(8,128)}, s32[]{:T(128)}, /*index=5*/s32[]{:T(128)}, s32[]{:T(128)}) while((s32[]{:T(128)}, f32[4,32,2048]{2,1,0:T(8,128)S(1)}, s32[8]{0:T(128)S(1)}, f32[4,32,8,2048]{3,1,0,2:T(8,128)}, s32[]{:T(128)}, ...), condition=%wide.region_1.2_spmd.clone, body=%wide.region_0.1_spmd.clone.sunk | while | flops 1114118 | bytes 6029450 | solution.py:31
  231.3 1.6 fusion.15
  232.9 0.6 dynamic_slice.14
  235.6 1.6 fusion.15
  239.9 1.6 fusion.15
  241.5 0.6 dynamic_slice.14
  244.1 1.6 fusion.15
  248.4 1.6 fusion.15
  250.0 0.6 dynamic_slice.14
  252.7 1.6 fusion.15
  254.3 0.6 dynamic_slice.14
  257.0 1.6 fusion.15
  261.2 1.6 fusion.15
  262.8 0.7 copy.19
  263.5 1.2 gather_fusion
  264.7 1.6 copy.21
  266.3 3.5 %all-to-all-start.1 = ((f32[4,8,1,4,2048]{4,1,3,2,0:T(8,128)}), f32[4,8,1,4,2048]{4,1,3,2,0:T(8,128)S(1)}, u32[]{:S(2)}, u32[]{:S(2)}) async-start(f32[4,8,1,4,2048]{4,1,3,2,0:T(8,128)} %copy.21), calls=%async_computation.1 | async-start | bytes 2097152 | tf_op jit(solution)/shard_map/all_to_all | solution.py:38
  269.8 0.7 slice_reduce_fusion
  270.5 20.1 %psum.7 = f32[]{:T(128)} all-reduce(f32[]{:T(128)} %slice_reduce_fusion), channel_id=1, replica_groups=mesh['frame'=4,'rank'=8] {'rank'}, use_global_device_ids=true, to_apply=%region_3.4 | all-reduce | flops 1 | bytes 8 | tf_op jit(solution)/shard_map/psum | solution.py:32
  291.7 1.6 copy.22
  (31 shorter events, 3.6 us)
Async XLA Ops:
  27.3 7.4 %copy-start = (s32[32]{0:T(128)S(1)}, s32[32]{0:T(128)}, u32[]{:S(2)}) copy-start(s32[32]{0:T(128)} %param.7) | copy-start | bytes 388
  27.3 190.6 %all-to-all-start = ((f32[8,4,32,1,2048]{4,3,2,1,0:T(1,128)}), f32[8,4,32,1,2048]{4,3,2,1,0:T(1,128)}, u32[]{:S(2)}, u32[]{:S(2)}) async-start(f32[8,4,32,1,2048]{4,3,2,1,0:T(1,128)} %fusion.2), calls=%async_computation | async-start | bytes 16777216 | tf_op jit(solution)/shard_map/all_to_all | solution.py:22
  217.9 10.7 %copy-start.1 = (s32[1,8]{1,0:T(1,128)S(1)}, s32[1,8]{1,0:T(1,128)}, u32[]{:S(2)}) copy-start(s32[1,8]{1,0:T(1,128)} %param.6) | copy-start | bytes 100
  266.3 24.9 %all-to-all-start.1 = ((f32[4,8,1,4,2048]{4,1,3,2,0:T(8,128)}), f32[4,8,1,4,2048]{4,1,3,2,0:T(8,128)S(1)}, u32[]{:S(2)}, u32[]{:S(2)}) async-start(f32[4,8,1,4,2048]{4,1,3,2,0:T(8,128)} %copy.21), calls=%async_computation.1 | async-start | bytes 2097152 | tf_op jit(solution)/shard_map/all_to_all | solution.py:38
